TPU v7x, 32 devices: a whole 2x2x4 slice. The times are simulated.
32 devices in a mesh: fsdp: 8 (over y, x, core), rep: 4 (over z).
Axes of the slice: x: 2, y: 2, z: 4, core: 2. Of those that a mesh axis runs over, the one named last changes fastest.
Arguments:
- hidden_in: bfloat16 [64, 512, 768], P(('fsdp', 'rep')), may hold values from -6 to 6
- lengths: int32 [64], P(('fsdp', 'rep')), may hold values from 128 to 512, as said below
- query_weight: bfloat16 [768, 768], P(('fsdp', 'rep')), may hold values from -0.21875 to 0.21875
- key_weight: bfloat16 [768, 768], P(('fsdp', 'rep')), may hold values from -0.21875 to 0.21875
- value_weight: bfloat16 [768, 768], P(('fsdp', 'rep')), may hold values from -0.21875 to 0.21875
- out_weight: bfloat16 [768, 768], P(('fsdp', 'rep')), may hold values from -3 to 3
- up_weight: bfloat16 [768, 3072], P(('fsdp', 'rep')), may hold values from -0.21875 to 0.21875
- down_weight: bfloat16 [3072, 768], P(('fsdp', 'rep')), may hold values from -0.109375 to 0.109375
- query_bias: bfloat16 [768], P(('fsdp', 'rep')), may hold values from -1.796875 to 1.796875
- value_bias: bfloat16 [768], P(('fsdp', 'rep')), may hold values from -1.796875 to 1.796875
- out_bias: bfloat16 [768], P(('fsdp', 'rep')), may hold values from -1.796875 to 1.796875
- up_bias: bfloat16 [3072], P(('fsdp', 'rep')), may hold values from -1.796875 to 1.796875
- down_bias: bfloat16 [768], P(('fsdp', 'rep')), may hold values from -1.796875 to 1.796875
- first_gain: bfloat16 [768], P(('fsdp', 'rep')), may hold values from 0.5 to 1.5
- first_shift: bfloat16 [768], P(('fsdp', 'rep')), may hold values from -1.796875 to 1.796875
- second_gain: bfloat16 [768], P(('fsdp', 'rep')), may hold values from 0.5 to 1.5
- second_shift: bfloat16 [768], P(('fsdp', 'rep')), may hold values from -1.796875 to 1.796875
- cotangent: bfloat16 [64, 512, 768], P(('fsdp', 'rep')), may hold values from -6 to 6
Outputs:
- hidden_out: bfloat16 [64, 512, 768], P(('fsdp', 'rep'))
- input_grad: bfloat16 [64, 512, 768], P(('fsdp', 'rep'))
- query_weight_grad: float32 [768, 768], P(('fsdp', 'rep'))
- key_weight_grad: float32 [768, 768], P(('fsdp', 'rep'))
- value_weight_grad: float32 [768, 768], P(('fsdp', 'rep'))
- out_weight_grad: float32 [768, 768], P(('fsdp', 'rep'))
- up_weight_grad: float32 [768, 3072], P(('fsdp', 'rep'))
- down_weight_grad: float32 [3072, 768], P(('fsdp', 'rep'))
- query_bias_grad: float32 [768], P(('fsdp', 'rep'))
- value_bias_grad: float32 [768], P(('fsdp', 'rep'))
- out_bias_grad: float32 [768], P(('fsdp', 'rep'))
- up_bias_grad: float32 [3072], P(('fsdp', 'rep'))
- down_bias_grad: float32 [768], P(('fsdp', 'rep'))
- first_gain_grad: float32 [768], P(('fsdp', 'rep'))
- first_shift_grad: float32 [768], P(('fsdp', 'rep'))
- second_gain_grad: float32 [768], P(('fsdp', 'rep'))
- second_shift_grad: float32 [768], P(('fsdp', 'rep'))
Inputs may be any that keep to these rules, and one draw needn't show every extreme that they name: `lengths`: one sequence fills all 512 slots and one has the fewest valid tokens.
All inputs are finite; a program needn't handle non-finite values.
Results may differ from a plain program's by a relative error of at most 0.015.
Values may be sent and summed in bfloat16 or wider, within the bound.
A program may use at most 192 MiB of HBM per device.

v0:
```python
import math

import jax
import jax.numpy as jnp
from jax import lax
from jax.sharding import PartitionSpec as P

H = 12
HD = 64


EPS = 1e-06


def gather_all(shards):
    whole = (
        lax.all_gather(shards[0], ("fsdp", "rep"), axis=0, tiled=True),
        lax.all_gather(shards[1], ("fsdp", "rep"), axis=0, tiled=True),
        lax.all_gather(shards[2], ("fsdp", "rep"), axis=0, tiled=True),
        lax.all_gather(shards[3], ("fsdp", "rep"), axis=0, tiled=True),
        lax.all_gather(shards[4], ("fsdp", "rep"), axis=0, tiled=True),
        lax.all_gather(shards[5], ("fsdp", "rep"), axis=0, tiled=True),
        lax.all_gather(shards[6], ("fsdp", "rep"), axis=0, tiled=True),
        lax.all_gather(shards[7], ("fsdp", "rep"), axis=0, tiled=True),
        lax.all_gather(shards[8], ("fsdp", "rep"), axis=0, tiled=True),
        lax.all_gather(shards[9], ("fsdp", "rep"), axis=0, tiled=True),
        lax.all_gather(shards[10], ("fsdp", "rep"), axis=0, tiled=True),
        lax.all_gather(shards[11], ("fsdp", "rep"), axis=0, tiled=True),
        lax.all_gather(shards[12], ("fsdp", "rep"), axis=0, tiled=True),
        lax.all_gather(shards[13], ("fsdp", "rep"), axis=0, tiled=True),
        lax.all_gather(shards[14], ("fsdp", "rep"), axis=0, tiled=True),
    )
    return whole


def reduce_all(terms):
    owned = (
        lax.psum_scatter(terms[0], ("fsdp", "rep"), scatter_dimension=0, tiled=True),
        lax.psum_scatter(terms[1], ("fsdp", "rep"), scatter_dimension=0, tiled=True),
        lax.psum_scatter(terms[2], ("fsdp", "rep"), scatter_dimension=0, tiled=True),
        lax.psum_scatter(terms[3], ("fsdp", "rep"), scatter_dimension=0, tiled=True),
        lax.psum_scatter(terms[4], ("fsdp", "rep"), scatter_dimension=0, tiled=True),
        lax.psum_scatter(terms[5], ("fsdp", "rep"), scatter_dimension=0, tiled=True),
        lax.psum_scatter(terms[6], ("fsdp", "rep"), scatter_dimension=0, tiled=True),
        lax.psum_scatter(terms[7], ("fsdp", "rep"), scatter_dimension=0, tiled=True),
        lax.psum_scatter(terms[8], ("fsdp", "rep"), scatter_dimension=0, tiled=True),
        lax.psum_scatter(terms[9], ("fsdp", "rep"), scatter_dimension=0, tiled=True),
        lax.psum_scatter(terms[10], ("fsdp", "rep"), scatter_dimension=0, tiled=True),
        lax.psum_scatter(terms[11], ("fsdp", "rep"), scatter_dimension=0, tiled=True),
        lax.psum_scatter(terms[12], ("fsdp", "rep"), scatter_dimension=0, tiled=True),
        lax.psum_scatter(terms[13], ("fsdp", "rep"), scatter_dimension=0, tiled=True),
        lax.psum_scatter(terms[14], ("fsdp", "rep"), scatter_dimension=0, tiled=True),
    )
    return owned


def matmul(left, right):
    return jnp.dot(left, right, preferred_element_type=jnp.float32)


def left_trans(left, right):
    return lax.dot_general(
        left, right, (((0,), (0,)), ((), ())), preferred_element_type=jnp.float32
    )


def right_trans(left, right):
    return lax.dot_general(
        left, right, (((1,), (1,)), ((), ())), preferred_element_type=jnp.float32
    )


def norm_forward(hidden, gain, shift):
    mean = jnp.mean(hidden, axis=-1, keepdims=True)
    centred = hidden - mean
    inverse = lax.rsqrt(jnp.mean(centred * centred, axis=-1, keepdims=True) + EPS)
    normed = centred * inverse
    return (normed * gain + shift, normed, inverse)


def norm_backward(grad_out, normed, inverse, gain):
    grad_normed = grad_out * gain
    grad_in = inverse * (
        grad_normed
        - jnp.mean(grad_normed, axis=-1, keepdims=True)
        - normed * jnp.mean(grad_normed * normed, axis=-1, keepdims=True)
    )
    return (grad_in, jnp.sum(grad_out * normed, axis=0), jnp.sum(grad_out, axis=0))


def head_scores(q_part, k_part, keep):
    raw = jnp.einsum("sqe,ske->sqk", q_part, k_part, preferred_element_type=jnp.float32) * (
        1.0 / math.sqrt(HD)
    )
    return jnp.where(keep[:, None, :], raw, -1e30)


def column_sums(grad):
    return jnp.sum(grad.astype(jnp.float32), axis=0)


def local(
    hidden_in,
    lengths,
    query_weight,
    key_weight,
    value_weight,
    out_weight,
    up_weight,
    down_weight,
    query_bias,
    value_bias,
    out_bias,
    up_bias,
    down_bias,
    first_gain,
    first_shift,
    second_gain,
    second_shift,
    cotangent,
):
    shards = (
        query_weight,
        key_weight,
        value_weight,
        out_weight,
        up_weight,
        down_weight,
        query_bias,
        value_bias,
        out_bias,
        up_bias,
        down_bias,
        first_gain,
        first_shift,
        second_gain,
        second_shift,
    )
    seqs, length, width = hidden_in.shape
    rows = seqs * length
    scale = 1.0 / math.sqrt(HD)
    keep = lax.broadcasted_iota(jnp.int32, (seqs, length), 1) < lengths[:, None]
    heads = jnp.arange(H, dtype=jnp.int32)
    whole = gather_all(shards)
    w_query, w_keys, w_values, w_out, w_up, w_down = whole[:6]
    b_query, b_values, b_out, b_up, b_down, gain_one, shift_one, gain_two, shift_two = [
        p.astype(jnp.float32) for p in whole[6:]
    ]
    inputs = hidden_in.reshape(rows, width)
    query = (matmul(inputs, w_query) + b_query).astype(jnp.bfloat16).reshape(seqs, length, width)
    keys = matmul(inputs, w_keys).astype(jnp.bfloat16).reshape(seqs, length, width)
    values = (matmul(inputs, w_values) + b_values).astype(jnp.bfloat16).reshape(seqs, length, width)

    def head_forward(head):
        start = head * HD
        q_part = lax.dynamic_slice_in_dim(query, start, HD, 2)
        k_part = lax.dynamic_slice_in_dim(keys, start, HD, 2)
        v_part = lax.dynamic_slice_in_dim(values, start, HD, 2)
        scores = head_scores(q_part, k_part, keep)
        peak = jnp.max(scores, axis=-1, keepdims=True)
        expo = jnp.exp(scores - peak)
        total = jnp.sum(expo, axis=-1, keepdims=True)
        probs = (expo / total).astype(jnp.bfloat16)
        mixed = jnp.einsum("sqk,ske->sqe", probs, v_part, preferred_element_type=jnp.float32)
        return (mixed.astype(jnp.bfloat16), (peak + jnp.log(total))[..., 0])

    head_out, log_sums = lax.map(head_forward, heads)
    context = jnp.transpose(head_out, (1, 2, 0, 3)).reshape(rows, width)
    first_sum = inputs.astype(jnp.float32) + matmul(context, w_out) + b_out
    first, normed_one, inverse_one = norm_forward(first_sum, gain_one, shift_one)
    first_low = first.astype(jnp.bfloat16)
    inner = matmul(first_low, w_up) + b_up
    active = jax.nn.gelu(inner, approximate=False).astype(jnp.bfloat16)
    second_sum = first + matmul(active, w_down) + b_down
    result, normed_two, inverse_two = norm_forward(second_sum, gain_two, shift_two)
    hidden_out = result.astype(jnp.bfloat16).reshape(seqs, length, width)
    again = gather_all(shards)
    w_query, w_keys, w_values, w_out, w_up, w_down = again[:6]
    gain_one = again[11].astype(jnp.float32)
    gain_two = again[13].astype(jnp.float32)
    grad_out = cotangent.reshape(rows, width).astype(jnp.float32)
    grad_second, grad_gain_two, grad_shift_two = norm_backward(
        grad_out, normed_two, inverse_two, gain_two
    )
    grad_branch = grad_second.astype(jnp.bfloat16)
    grad_b_down = column_sums(grad_branch)
    grad_w_down = left_trans(active, grad_branch)
    grad_active = right_trans(grad_branch, w_down)
    gelu_value, gelu_pull = jax.vjp(lambda z: jax.nn.gelu(z, approximate=False), inner)
    grad_inner = gelu_pull(grad_active)[0].astype(jnp.bfloat16)
    grad_b_up = column_sums(grad_inner)
    grad_w_up = left_trans(first_low, grad_inner)
    grad_first = grad_second + right_trans(grad_inner, w_up)
    grad_first_sum, grad_gain_one, grad_shift_one = norm_backward(
        grad_first, normed_one, inverse_one, gain_one
    )
    grad_attn = grad_first_sum.astype(jnp.bfloat16)
    grad_b_out = column_sums(grad_attn)
    grad_w_out = left_trans(context, grad_attn)
    grad_context = right_trans(grad_attn, w_out).astype(jnp.bfloat16).reshape(seqs, length, width)

    def head_backward(pair):
        head, log_sum = pair
        start = head * HD
        q_part = lax.dynamic_slice_in_dim(query, start, HD, 2)
        k_part = lax.dynamic_slice_in_dim(keys, start, HD, 2)
        v_part = lax.dynamic_slice_in_dim(values, start, HD, 2)
        g_part = lax.dynamic_slice_in_dim(grad_context, start, HD, 2)
        scores = head_scores(q_part, k_part, keep)
        probs_full = jnp.exp(scores - log_sum[..., None])
        probs = probs_full.astype(jnp.bfloat16)
        grad_probs = jnp.einsum("sqe,ske->sqk", g_part, v_part, preferred_element_type=jnp.float32)
        grad_v = jnp.einsum("sqk,sqe->ske", probs, g_part, preferred_element_type=jnp.float32)
        grad_scores = probs_full * (
            grad_probs - jnp.sum(grad_probs * probs_full, axis=-1, keepdims=True)
        )
        grad_low = grad_scores.astype(jnp.bfloat16)
        grad_q = (
            jnp.einsum("sqk,ske->sqe", grad_low, k_part, preferred_element_type=jnp.float32) * scale
        )
        grad_k = (
            jnp.einsum("sqk,sqe->ske", grad_low, q_part, preferred_element_type=jnp.float32) * scale
        )
        return (
            grad_q.astype(jnp.bfloat16),
            grad_k.astype(jnp.bfloat16),
            grad_v.astype(jnp.bfloat16),
        )

    head_q, head_k, head_v = lax.map(head_backward, (heads, log_sums))
    grad_query = jnp.transpose(head_q, (1, 2, 0, 3)).reshape(rows, width)
    grad_keys = jnp.transpose(head_k, (1, 2, 0, 3)).reshape(rows, width)
    grad_values = jnp.transpose(head_v, (1, 2, 0, 3)).reshape(rows, width)
    grad_input = (
        grad_first_sum
        + right_trans(grad_query, w_query)
        + right_trans(grad_keys, w_keys)
        + right_trans(grad_values, w_values)
    )
    input_grad = grad_input.astype(jnp.bfloat16).reshape(seqs, length, width)
    terms = (
        left_trans(inputs, grad_query),
        left_trans(inputs, grad_keys),
        left_trans(inputs, grad_values),
        grad_w_out,
        grad_w_up,
        grad_w_down,
        column_sums(grad_query),
        column_sums(grad_values),
        grad_b_out,
        grad_b_up,
        grad_b_down,
        grad_gain_one,
        grad_shift_one,
        grad_gain_two,
        grad_shift_two,
    )
    owned = reduce_all(terms)
    return (
        hidden_out,
        input_grad,
        owned[0],
        owned[1],
        owned[2],
        owned[3],
        owned[4],
        owned[5],
        owned[6],
        owned[7],
        owned[8],
        owned[9],
        owned[10],
        owned[11],
        owned[12],
        owned[13],
        owned[14],
    )


def solution(mesh):
    in_specs = (
        P(("fsdp", "rep"), None, None),
        P(("fsdp", "rep")),
        P(("fsdp", "rep"), None),
        P(("fsdp", "rep"), None),
        P(("fsdp", "rep"), None),
        P(("fsdp", "rep"), None),
        P(("fsdp", "rep"), None),
        P(("fsdp", "rep"), None),
        P(("fsdp", "rep")),
        P(("fsdp", "rep")),
        P(("fsdp", "rep")),
        P(("fsdp", "rep")),
        P(("fsdp", "rep")),
        P(("fsdp", "rep")),
        P(("fsdp", "rep")),
        P(("fsdp", "rep")),
        P(("fsdp", "rep")),
        P(("fsdp", "rep"), None, None),
    )
    out_specs = (
        P(("fsdp", "rep"), None, None),
        P(("fsdp", "rep"), None, None),
        P(("fsdp", "rep"), None),
        P(("fsdp", "rep"), None),
        P(("fsdp", "rep"), None),
        P(("fsdp", "rep"), None),
        P(("fsdp", "rep"), None),
        P(("fsdp", "rep"), None),
        P(("fsdp", "rep")),
        P(("fsdp", "rep")),
        P(("fsdp", "rep")),
        P(("fsdp", "rep")),
        P(("fsdp", "rep")),
        P(("fsdp", "rep")),
        P(("fsdp", "rep")),
        P(("fsdp", "rep")),
        P(("fsdp", "rep")),
    )
    return jax.shard_map(local, mesh=mesh, in_specs=in_specs, out_specs=out_specs, check_vma=False)
```

profile of v0, /device:TPU:0, one launch (start us, length us, event | category | flops | bytes accessed | tf_op | source)
XLA Modules:
  0.0 1172.2 jit_solution(12067138237935054540)
XLA Ops:
  18.8 42.5 %all-reduce.19 = (bf16[768]{0:T(1024)(128)(2,1)S(1)}, bf16[768]{0:T(1024)(128)(2,1)S(1)}, bf16[768]{0:T(1024)(128)(2,1)S(1)}, bf16[768]{0:T(1024)(128)(2,1)S(1)}...) all-reduce(bf16[768]{0:T(1024)(128)(2,1)S(1)} %dynamic-update-slice, ...), channel_id=1, replica_groups=mesh['fsdp'=8,'rep'=4] {'fsdp','rep'}, use_global_device_ids=true, to_apply=%add | all-reduce | flops 9216 | bytes 36864
  61.3 2.7 convert_reduce_fusion.1
  64.1 3.7 all-gather.7.cloned.1.call-done
  67.8 3.1 add_convert_fusion.4
  71.6 52.1 %all-gather.11.cloned.1.call-done = bf16[768,768]{1,0:T(8,128)(2,1)} async-done(((bf16[24,768]{1,0:T(8,128)(2,1)}), bf16[768,768]{1,0:T(8,128)(2,1)}) %all-gather.11.cloned.1.call-update) | async-done | bytes 1179664 | tf_op jit(solution)/shard_map/all_gather | solution.py:19
  123.8 3.1 add_convert_fusion.3
  128.5 51.0 %all-gather.9.cloned.1.call-done = bf16[768,768]{1,0:T(8,128)(2,1)} async-done(((bf16[24,768]{1,0:T(8,128)(2,1)}), bf16[768,768]{1,0:T(8,128)(2,1)}) %all-gather.9.cloned.1.call-update) | async-done | bytes 1179664 | tf_op jit(solution)/shard_map/all_gather | solution.py:18
  179.5 3.1 convolution_convert_fusion.3
  184.4 65.9 %while.28 = (s32[]{:T(128)}, bf16[12,2,512,64]{2,3,1,0:T(8,128)(2,1)S(1)}, f32[12,2,512]{2,1,0:T(2,128)}, s32[12]{0:T(128)S(1)}, bf16[2,512,768]{1,2,0:T(8,128)(...) while((s32[]{:T(128)}, ...), condition=%wide.region_3.4_spmd.clone, body=%wide.region_0.3_spmd.clone.sunk | while | flops 140574720 | bytes 6856891 | solution.py:167
  253.6 3.9 fusion.65
  258.0 42.5 %all-gather.15.cloned.1.call-done = bf16[768,3072]{1,0:T(8,128)(2,1)} async-done(((bf16[24,3072]{1,0:T(8,128)(2,1)}), bf16[768,3072]{1,0:T(8,128)(2,1)}) %all-gather.15.cloned.1.call-update) | async-done | bytes 4718608 | tf_op jit(solution)/shard_map/all_gather | solution.py:21
  300.4 36.0 %multiply_convert_fusion.1 = (bf16[1024,3072]{1,0:T(8,128)(2,1)}, f32[1024,3072]{1,0:T(8,128)}, f32[1024,3072]{1,0:T(8,128)}) fusion(f32[3072]{0:T(1024)S(1)} %convert_element_type.123, bf16[768,3072]{1,0:T(8,128)(2,1)} %all-gather.15.cloned.1.call-done, f32[1024,768]{1,0:T(8,128)S(1)} %get-tuple-element.352, f32[768]{0:T(1024)S(1)} %convert_element_type.121, ...), kind=kOutput, calls=%fused_computation.55 | convolution fusion | flops 5043388416 | bytes 39348224 | tf_op jit(solution)/shard_map/dot_general | solution.py:58
  336.5 28.5 %all-gather.17.cloned.1.call-done = bf16[3072,768]{1,0:T(8,128)(2,1)} async-done(((bf16[96,768]{1,0:T(8,128)(2,1)}), bf16[3072,768]{1,0:T(8,128)(2,1)}) %all-gather.17.cloned.1.call-update) | async-done | bytes 4718608 | tf_op jit(solution)/shard_map/all_gather | solution.py:22
  365.0 8.8 fusion.66
  376.5 2.9 convert_reduce_fusion.2
  379.4 19.1 %convert_reduce_fusion = (f32[3072]{0:T(1024)S(1)}, bf16[1024,3072]{1,0:T(8,128)(2,1)}) fusion(f32[1024,3072]{1,0:T(8,128)} %get-tuple-element.345, bf16[3072,768]{1,0:T(8,128)(2,1)} %all-gather.17.cloned.1.call-done, f32[1024,768]{1,0:T(8,128)} %get-tuple-element.341, f32[1024,3072]{1,0:T(8,128)} %get-tuple-element.353, f32[3072]{0:T(1024)S(1)} %convert_element_type.123), kind=kOutput, calls=%fused_computation.53 | convolution fusion | flops 4886098944 | bytes 39346176 | tf_op jit(solution)/shard_map/dot_general | solution.py:68
  398.5 10.0 multiply_reduce_fusion.1
  411.3 2.9 fusion.53
  414.2 4.8 convolution_convert_fusion.2
  419.0 2.6 copy.77
  425.7 138.3 %while.29 = (s32[]{:T(128)}, bf16[12,2,512,64]{2,3,1,0:T(8,128)(2,1)}, bf16[12,2,512,64]{2,3,1,0:T(8,128)(2,1)}, bf16[12,2,512,64]{2,3,1,0:T(8,128)(2,1)}, s32[1...) while((s32[]{:T(128)}, ...), condition=%wide.region_14.15_spmd.clone, body=%wide.region_12.14_spmd.clone.sunk | while | flops 340590592 | bytes 17065696 | solution.py:230
  431.6 2.0 fusion.129
  435.4 2.0 fusion.130
  443.1 2.0 fusion.129
  446.9 2.0 fusion.130
  454.6 2.0 fusion.129
  456.6 1.9 fusion.128
  458.5 2.0 fusion.130
  466.1 2.0 fusion.129
  470.0 2.0 fusion.130
  477.7 2.0 fusion.129
  481.5 2.0 fusion.130
  489.2 2.0 fusion.129
  493.0 2.0 fusion.130
  500.7 2.0 fusion.129
  504.5 2.0 fusion.130
  512.2 2.0 fusion.129
  516.0 2.0 fusion.130
  523.7 2.0 fusion.129
  527.5 2.0 fusion.130
  535.2 2.0 fusion.129
  539.1 2.0 fusion.130
  546.7 2.0 fusion.129
  550.5 2.0 fusion.130
  558.2 2.0 fusion.129
  562.0 2.0 fusion.130
  564.0 3.1 copy.79
  568.7 2.8 convolution_bitcast_fusion.2
  571.6 3.0 copy.89
  574.7 3.1 copy.80
  579.4 2.8 convolution_bitcast_fusion.1
  582.3 3.1 copy.91
  585.7 3.2 copy.81
  590.4 2.9 convolution_bitcast_fusion
  593.3 3.1 copy.93
  596.5 10.7 fusion.59
  609.2 10.2 fusion.56
  622.9 40.4 %all-reduce.18 = (f32[768]{0:T(1024)S(1)}, f32[768]{0:T(1024)S(1)}, f32[768]{0:T(1024)S(1)}, f32[3072]{0:T(1024)S(1)}, f32[768]{0:T(1024)S(1)}, /*index=5*/f32[7...) all-reduce(f32[768]{0:T(1024)S(1)} %reduce_sum.184, ...), channel_id=8, replica_groups=mesh['fsdp'=8,'rep'=4] {'fsdp','rep'}, use_global_device_ids=true, to_apply=%region_22.23.clone | all-reduce | flops 9216 | bytes 73728
  668.6 2.9 fusion.67
  674.2 2.7 add_convert_fusion.1
  677.0 100.3 %reduce-scatter.21.cloned.1.call-done = f32[24,768]{1,0:T(8,128)} async-done(((f32[768,768]{1,0:T(8,128)}), f32[24,768]{1,0:T(8,128)}) %reduce-scatter.21.cloned.1.call-update) | async-done | bytes 73744
  777.3 104.4 %reduce-scatter.23.cloned.1.call-done = f32[24,768]{1,0:T(8,128)} async-done(((f32[768,768]{1,0:T(8,128)}), f32[24,768]{1,0:T(8,128)}) %reduce-scatter.23.cloned.1.call-update) | async-done | bytes 73744
  881.7 141.7 %reduce-scatter.15.cloned.1.call-done = f32[24,3072]{1,0:T(8,128)} async-done(((f32[768,3072]{1,0:T(8,128)}), f32[24,3072]{1,0:T(8,128)}) %reduce-scatter.15.cloned.1.call-update) | async-done | bytes 294928 | tf_op jit(solution)/shard_map/reduce_scatter | solution.py:42
  1023.4 141.5 %reduce-scatter.17.cloned.1.call-done = f32[96,768]{1,0:T(8,128)} async-done(((f32[3072,768]{1,0:T(8,128)}), f32[96,768]{1,0:T(8,128)}) %reduce-scatter.17.cloned.1.call-update) | async-done | bytes 294928 | tf_op jit(solution)/shard_map/reduce_scatter | solution.py:43
  (292 shorter events, 185.1 us)
Async XLA Ops:
  7.2 60.6 %all-gather.7.cloned.1.call-start = ((), (), s32[]{:S(2)}) async-start(), calls=%async_computation.6 | async-start | bytes 1216512 | tf_op jit(solution)/shard_map/all_gather | solution.py:17
  7.9 115.8 %all-gather.11.cloned.1.call-start = ((), (), s32[]{:S(2)}) async-start(), calls=%async_computation.8 | async-start | bytes 1216512 | tf_op jit(solution)/shard_map/all_gather | solution.py:19
  8.7 170.8 %all-gather.9.cloned.1.call-start = ((), (), s32[]{:S(2)}) async-start(), calls=%async_computation.7 | async-start | bytes 1216512 | tf_op jit(solution)/shard_map/all_gather | solution.py:18
  9.4 244.2 %all-gather.13.cloned.1.call-start = ((), (), s32[]{:S(2)}) async-start(), calls=%async_computation.9 | async-start | bytes 1216512 | tf_op jit(solution)/shard_map/all_gather | solution.py:20
  10.0 290.5 %all-gather.15.cloned.1.call-start = ((), (), s32[]{:S(2)}) async-start(), calls=%async_computation.10 | async-start | bytes 4866048 | tf_op jit(solution)/shard_map/all_gather | solution.py:21
  10.6 354.4 %all-gather.17.cloned.1.call-start = ((), (), s32[]{:S(2)}) async-start(), calls=%async_computation.11 | async-start | bytes 4866048 | tf_op jit(solution)/shard_map/all_gather | solution.py:22
  11.1 665.8 %reduce-scatter.13.cloned.1.call-start = ((), (), s32[]{:S(2)}) async-start(), calls=%async_computation.12 | async-start | bytes 2433024 | tf_op jit(solution)/shard_map/reduce_scatter | solution.py:41
  182.6 1.8 copy-start.14
  250.3 3.3 copy-start.6
  373.8 1.4 copy-start
  408.5 2.8 copy-start.12
  409.6 1.7 copy-start.2
  421.6 4.1 copy-start.15
  421.6 255.3 %reduce-scatter.19.cloned.1.call-start = ((), (), s32[]{:S(2)}) async-start(), calls=%async_computation.15 | async-start | bytes 2433024
  564.0 4.7 copy-start.17
  567.6 1.1 copy-start.8
  574.7 202.6 %reduce-scatter.21.cloned.1.call-start = ((), (), s32[]{:S(2)}) async-start(), calls=%async_computation.16 | async-start | bytes 2433024
  574.7 4.7 copy-start.18
  578.3 1.1 copy-start.10
  585.4 296.3 %reduce-scatter.23.cloned.1.call-start = ((), (), s32[]{:S(2)}) async-start(), calls=%async_computation.17 | async-start | bytes 2433024
  585.7 4.7 copy-start.19
  589.3 1.1 copy-start.4
  596.4 426.9 %reduce-scatter.15.cloned.1.call-start = ((), (), s32[]{:S(2)}) async-start(), calls=%async_computation.13 | async-start | bytes 9732096 | tf_op jit(solution)/shard_map/reduce_scatter | solution.py:42
  607.2 1.9 copy-start.7
  607.2 557.6 %reduce-scatter.17.cloned.1.call-start = ((), (), s32[]{:S(2)}) async-start(), calls=%async_computation.14 | async-start | bytes 9732096 | tf_op jit(solution)/shard_map/reduce_scatter | solution.py:43
  619.4 1.4 copy-start.1
  619.4 3.5 copy-start.16
  619.4 49.2 %copy-start.9 = (bf16[96,8,2,512]{3,1,2,0:T(8,128)(2,1)S(1)}, bf16[96,8,2,512]{3,1,2,0:T(8,128)(2,1)}, u32[]{:S(2)}) copy-start(bf16[96,8,2,512]{3,1,2,0:T(8,128)(2,1)} %copy-done.8) | copy-start | bytes 4718596
  668.6 2.9 copy-start.11
  668.6 2.9 copy-start.20
  671.5 1.9 copy-start.3
  671.5 2.4 copy-start.5
  671.6 2.7 copy-start.13
Sparse Core Ops, SparseCore 0:
  10.8 56.9 all-gather.6
  70.6 53.1 all-gather.10
  126.6 52.9 all-gather.8
  182.2 52.9 all-gather.12
  237.8 62.5 all-gather.14
  303.1 61.8 all-gather.16
  421.8 98.0 reduce-scatter.12
  574.8 97.9 reduce-scatter.18
  678.6 98.6 reduce-scatter.20
  783.0 98.6 reduce-scatter.22
  888.2 135.1 reduce-scatter.14
  1029.7 135.1 reduce-scatter.16
where the time goes:
time: 1180 us; the launch traced here: 1170 us
  waiting for transfers between devices  669 us (57%)
  matrix products  275 us (23%)
  blocking collectives  82.9 us (7%)
  local copies, waits for them, and re-layouts  79.6 us (7%)
  other arithmetic  33 us (3%)
  loops' own time  16.4 us (1%)
  between operations  15.1 us (1%)
    unnamed x15, waiting for transfers between devices  208 us
    reduce_scatter x1, waiting for transfers between devices, reduce_all(): lax.psum_scatter(terms[4], ('fsdp', 'rep'), scatter_dimension=0, tiled=True)  142 us
    reduce_scatter x1, waiting for transfers between devices, reduce_all(): lax.psum_scatter(terms[5], ('fsdp', 'rep'), scatter_dimension=0, tiled=True)  142 us
    unnamed x2, blocking collectives  82.9 us
    dot_general x6, matrix products, matmul(): return jnp.dot(left, right, preferred_element_type=jnp.float32)  58.1 us
    all_gather x1, waiting for transfers between devices, gather_all(): lax.all_gather(shards[2], ('fsdp', 'rep'), axis=0, tiled=True)  52.1 us
    all_gather x1, waiting for transfers between devices, gather_all(): lax.all_gather(shards[1], ('fsdp', 'rep'), axis=0, tiled=True)  51 us
    all_gather x1, waiting for transfers between devices, gather_all(): lax.all_gather(shards[4], ('fsdp', 'rep'), axis=0, tiled=True)  42.5 us
  transfers between devices with their start and end apart: 12, of which 9 were waited for; matrix products, arithmetic and copies ran while one was open for 28% of the time, Pallas kernels for 0%

commit v1 on v0

v1 whole, which is shorter than its diff:
```python
import functools
import math

import jax
import jax.numpy as jnp
from jax import lax
from jax.experimental import pallas as pl
from jax.experimental.pallas import tpu as pltpu
from jax.sharding import PartitionSpec as P

HD = 64
PAIR = 2 * HD
BF = jnp.bfloat16
F32 = jnp.float32


def nt(left, right):
    return lax.dot_general(left, right, (((1,), (1,)), ((), ())), preferred_element_type=F32)


def nn(left, right):
    return jnp.dot(left, right, preferred_element_type=F32)


def tn(left, right):
    return lax.dot_general(left, right, (((0,), (0,)), ((), ())), preferred_element_type=F32)


def head_masks(length):
    lane = lax.broadcasted_iota(jnp.int32, (length, PAIR), 1)
    return lane


def masked_keys(k2, lane, head, valid):
    inside = (lane // HD) == head
    slot = lane == (1 - head) * HD
    row = lax.broadcasted_iota(jnp.int32, lane.shape, 0)
    bias = jnp.where(row < valid, 0.0, -1e30).astype(BF)
    return jnp.where(inside, k2, jnp.where(slot, bias, jnp.zeros_like(k2)))


def masked_query(q2, lane, head):
    inside = (lane // HD) == head
    slot = lane == (1 - head) * HD
    return jnp.where(inside, q2, jnp.where(slot, jnp.ones_like(q2), jnp.zeros_like(q2)))


def attention_forward_kernel(chunk, len_ref, q_ref, k_ref, v_ref, ctx_ref, lse_ref):
    valid = len_ref[pl.program_id(0)]
    length = q_ref.shape[0]
    lane = head_masks(length)
    first_c = lax.broadcasted_iota(jnp.int32, (chunk, PAIR), 1) < HD
    lane_c = lax.broadcasted_iota(jnp.int32, (chunk, PAIR), 1)
    k2, v2 = k_ref[...], v_ref[...]
    km = [masked_keys(k2, lane, h, valid) for h in (0, 1)]
    vm = [jnp.where((lane // HD) == h, v2, jnp.ones_like(v2)) for h in (0, 1)]
    for c in range(length // chunk):
        rows = pl.ds(c * chunk, chunk)
        q2 = q_ref[rows, :] * BF(0.125)
        outs, tops = [], []
        for h in (0, 1):
            s = nt(masked_query(q2, lane_c, h), km[h])
            top = jnp.max(s, axis=1, keepdims=True)
            e = jnp.exp(s - top).astype(BF)
            outs.append(nn(e, vm[h]))
            tops.append(top)
        num = jnp.where(first_c, outs[0], outs[1])
        den = pltpu.roll(jnp.where(first_c, outs[1], outs[0]), HD, 1)
        ctx_ref[rows, :] = (num / den).astype(BF)
        lse = jnp.where(first_c, tops[0], tops[1]) + jnp.log(den)
        turned = lse.T
        lse_ref[0, 0, 0:1, rows] = turned[0:1]
        lse_ref[0, 0, 1:2, rows] = turned[HD : HD + 1]


def attention_forward(lengths, qkv, seqs, length, width, chunk=512):
    pairs = width // PAIR
    return pl.pallas_call(
        functools.partial(attention_forward_kernel, chunk),
        grid_spec=pltpu.PrefetchScalarGridSpec(
            num_scalar_prefetch=1,
            grid=(seqs, pairs),
            in_specs=[
                pl.BlockSpec((length, PAIR), lambda s, p, n: (s, p)),
                pl.BlockSpec((length, PAIR), lambda s, p, n: (s, pairs + p)),
                pl.BlockSpec((length, PAIR), lambda s, p, n: (s, 2 * pairs + p)),
            ],
            out_specs=[
                pl.BlockSpec((length, PAIR), lambda s, p, n: (s, p)),
                pl.BlockSpec((1, 1, 2, length), lambda s, p, n: (s, p, 0, 0)),
            ],
        ),
        out_shape=[
            jax.ShapeDtypeStruct((seqs * length, width), BF),
            jax.ShapeDtypeStruct((seqs, pairs, 2, length), F32),
        ],
        name="attention_forward",
    )(lengths, qkv, qkv, qkv)


def attention_backward_kernel(chunk, len_ref, q_ref, k_ref, v_ref, g_ref, ctx_ref, lse_ref, dq_ref, dk_ref, dv_ref):
    valid = len_ref[pl.program_id(0)]
    length = q_ref.shape[0]
    lane = head_masks(length)
    first = lane < HD
    q2 = q_ref[...] * BF(0.125)
    g2 = g_ref[...]
    k2, v2 = k_ref[...], v_ref[...]
    k8 = k2 * BF(0.125)
    turned = (g2.astype(F32) * ctx_ref[...].astype(F32)).T
    dqs, dks, dvs = [], [], []
    for h in (0, 1):
        km = masked_keys(k2, lane, h, valid)
        qm = masked_query(q2, lane, h)
        vm = jnp.where((lane // HD) == h, v2, jnp.zeros_like(v2))
        delta = jnp.sum(turned[h * HD : (h + 1) * HD], axis=0, keepdims=True)
        lse = lse_ref[0, 0, h : h + 1, :]
        dk_parts, dv_parts, dq = [], [], None
        for c in range(length // chunk):
            rows = slice(c * chunk, (c + 1) * chunk)
            p = jnp.exp(nt(km[rows], qm) - lse)
            ds = (p * (nt(vm[rows], g2) - delta)).astype(BF)
            dv_parts.append(nn(p.astype(BF), g2))
            dk_parts.append(nn(ds, q2))
            part = tn(ds, k8[rows])
            dq = part if dq is None else dq + part
        dqs.append(dq)
        dks.append(jnp.concatenate(dk_parts, 0))
        dvs.append(jnp.concatenate(dv_parts, 0))
    dq_ref[...] = jnp.where(first, dqs[0], dqs[1]).astype(BF)
    dk_ref[...] = jnp.where(first, dks[0], dks[1]).astype(BF)
    dv_ref[...] = jnp.where(first, dvs[0], dvs[1]).astype(BF)


def attention_backward(lengths, qkv, grad, ctx, lse, seqs, length, width, chunk=512):
    pairs = width // PAIR
    col = lambda k: pl.BlockSpec((length, PAIR), lambda s, p, n: (s, k * pairs + p))
    return pl.pallas_call(
        functools.partial(attention_backward_kernel, chunk),
        grid_spec=pltpu.PrefetchScalarGridSpec(
            num_scalar_prefetch=1,
            grid=(seqs, pairs),
            in_specs=[col(0), col(1), col(2), col(0), col(0), pl.BlockSpec((1, 1, 2, length), lambda s, p, n: (s, p, 0, 0))],
            out_specs=[col(0), col(0), col(0)],
        ),
        out_shape=[jax.ShapeDtypeStruct((seqs * length, width), BF)] * 3,
        name="attention_backward",
    )(lengths, qkv, qkv, qkv, grad, ctx, lse)


def gather(mesh_shape, pieces):
    return gather_native(pieces)


def reduce(mesh_shape, terms):
    return reduce_native(terms)


EPS = 1e-06
AXES = ("fsdp", "rep")


def norm_forward(hidden, gain, shift):
    mean = jnp.mean(hidden, axis=-1, keepdims=True)
    centred = hidden - mean
    inverse = lax.rsqrt(jnp.mean(centred * centred, axis=-1, keepdims=True) + EPS)
    normed = centred * inverse
    return (normed * gain + shift, normed, inverse)


def norm_backward(grad_out, normed, inverse, gain):
    grad_normed = grad_out * gain
    grad_in = inverse * (
        grad_normed
        - jnp.mean(grad_normed, axis=-1, keepdims=True)
        - normed * jnp.mean(grad_normed * normed, axis=-1, keepdims=True)
    )
    return (grad_in, jnp.sum(grad_out * normed, axis=0), jnp.sum(grad_out, axis=0))


def column_sums(grad):
    return jnp.sum(grad.astype(F32), axis=0)


def gather_native(pieces):
    return [lax.all_gather(p, AXES, axis=0, tiled=False) for p in pieces]


def reduce_native(terms):
    return [lax.psum_scatter(t.astype(F32), AXES, scatter_dimension=0, tiled=False) for t in terms]


def local(
    mesh_shape,
    hidden_in,
    lengths,
    query_weight,
    key_weight,
    value_weight,
    out_weight,
    up_weight,
    down_weight,
    query_bias,
    value_bias,
    out_bias,
    up_bias,
    down_bias,
    first_gain,
    first_shift,
    second_gain,
    second_shift,
    cotangent,
):
    seqs, length, width = hidden_in.shape
    rows = seqs * length
    hidden = up_weight.shape[1]
    share = query_weight.shape[0]
    spread = hidden // width
    devices = width // share
    vectors = jnp.concatenate(
        [
            jnp.stack([query_bias, value_bias, out_bias, down_bias, first_gain, first_shift, second_gain, second_shift]),
            up_bias.reshape(spread, share),
        ]
    )
    count = vectors.shape[0]
    vector_slot = jnp.pad(vectors, ((0, -count % 16), (0, -share % 128)))
    qkv_shard = jnp.concatenate([query_weight, key_weight, value_weight], axis=1)
    got = gather(mesh_shape, [vector_slot, qkv_shard, out_weight, up_weight, down_weight])
    w_qkv = got[1].reshape(width, 3 * width)
    w_out = got[2].reshape(width, width)
    w_up = got[3].reshape(width, hidden)
    w_down = got[4].reshape(hidden, width)
    wide = got[0].astype(F32)
    plain = jnp.transpose(wide[:, :8, :share], (1, 0, 2)).reshape(8, width)
    b_query, b_values, b_out, b_down, gain_one, shift_one, gain_two, shift_two = [plain[i] for i in range(8)]
    b_up = wide[:, 8 : 8 + spread, :share].reshape(hidden)

    inputs = hidden_in.reshape(rows, width)
    b_qkv = jnp.concatenate([b_query, jnp.zeros_like(b_query), b_values])
    qkv = (nn(inputs, w_qkv) + b_qkv).astype(BF)
    context, log_sums = attention_forward(lengths, qkv, seqs, length, width)
    first_sum = inputs.astype(F32) + nn(context, w_out) + b_out
    first, normed_one, inverse_one = norm_forward(first_sum, gain_one, shift_one)
    first_low = first.astype(BF)
    inner = nn(first_low, w_up) + b_up
    half = 0.5 * (1.0 + lax.erf(inner * (2.0**-0.5)))
    active = (inner * half).astype(BF)
    slope = half + inner * ((2.0 * math.pi) ** -0.5) * jnp.exp(-0.5 * inner * inner)
    slope = slope.astype(BF)
    second_sum = first + nn(active, w_down) + b_down
    result, normed_two, inverse_two = norm_forward(second_sum, gain_two, shift_two)
    hidden_out = result.astype(BF).reshape(seqs, length, width)
    grad_out = cotangent.reshape(rows, width).astype(F32)
    grad_second, grad_gain_two, grad_shift_two = norm_backward(grad_out, normed_two, inverse_two, gain_two)
    grad_branch = grad_second.astype(BF)
    grad_b_down = column_sums(grad_branch)
    grad_w_down = tn(active, grad_branch)
    grad_active = nt(grad_branch, w_down)
    grad_inner = (grad_active * slope.astype(F32)).astype(BF)
    grad_b_up = column_sums(grad_inner)
    grad_w_up = tn(first_low, grad_inner)
    grad_first = grad_second + nt(grad_inner, w_up)
    grad_first_sum, grad_gain_one, grad_shift_one = norm_backward(grad_first, normed_one, inverse_one, gain_one)
    grad_attn = grad_first_sum.astype(BF)
    grad_b_out = column_sums(grad_attn)
    grad_w_out = tn(context, grad_attn)
    grad_context = nt(grad_attn, w_out).astype(BF)
    grad_query, grad_keys, grad_values = attention_backward(
        lengths, qkv, grad_context, context, log_sums, seqs, length, width
    )
    grad_qkv = jnp.concatenate([grad_query, grad_keys, grad_values], axis=1)
    input_grad = (grad_first_sum + nt(grad_qkv, w_qkv)).astype(BF).reshape(seqs, length, width)
    grad_w_qkv = tn(inputs, grad_qkv)
    sums = jnp.stack(
        [
            column_sums(grad_query),
            column_sums(grad_values),
            grad_b_out,
            grad_b_down,
            grad_gain_one,
            grad_shift_one,
            grad_gain_two,
            grad_shift_two,
        ]
    )
    vector_terms = jnp.concatenate(
        [jnp.transpose(sums.reshape(8, devices, share), (1, 0, 2)), grad_b_up.reshape(devices, spread, share)], axis=1
    )
    vector_terms = jnp.pad(vector_terms, ((0, 0), (0, -count % 16), (0, -share % 128)))
    owned = reduce(
        mesh_shape,
        [
            vector_terms,
            grad_w_qkv.reshape(devices, share, 3 * width),
            grad_w_out.reshape(devices, share, width),
            grad_w_up.reshape(devices, share, hidden),
            grad_w_down.reshape(devices, spread * share, width),
        ],
    )
    vec = owned[0][:count, :share]
    return (
        hidden_out,
        input_grad,
        owned[1][:, :width],
        owned[1][:, width : 2 * width],
        owned[1][:, 2 * width :],
        owned[2],
        owned[3],
        owned[4],
        vec[0],
        vec[1],
        vec[2],
        vec[8:].reshape(spread * share),
        vec[3],
        vec[4],
        vec[5],
        vec[6],
        vec[7],
    )


def solution(mesh):
    rows = P(AXES, None)
    flat = P(AXES)
    cube = P(AXES, None, None)
    in_specs = (cube, flat) + (rows,) * 6 + (flat,) * 9 + (cube,)
    out_specs = (cube, cube) + (rows,) * 6 + (flat,) * 9
    body = functools.partial(local, dict(mesh.shape))
    return jax.shard_map(body, mesh=mesh, in_specs=in_specs, out_specs=out_specs, check_vma=False)
```

time: 1180 us -> 979 us (0.83)
  matrix products: 275 us -> 97 us
  local copies, waits for them, and re-layouts: 79.6 us -> 20.8 us
  waiting for transfers between devices: 669 us -> 721 us
  Pallas kernels: 0 us -> 40.2 us
  other arithmetic: 33 us -> 12.9 us
  loops' own time: 16.4 us -> 0 us
  blocking collectives: 82.9 us -> 71 us
    reduce_scatter x3 -> x5, waiting for transfers between devices: 283 us -> 588 us  [reduce_native(): lax.psum_scatter(t.astype(F32), AXES, scatter_dimension=0, tiled=False)]
    unnamed x15 -> x9, waiting for transfers between devices: 208 us -> 2 us
    dot_general x102 -> x12, matrix products: 275 us -> 97 us  [the longest x4 34.4 us: tn(): lax.dot_general(left, right, (((0,), (0,)), ((), ())), preferred_element_...]
    unnamed x2 -> x0, blocking collectives: 82.9 us -> none
    all_gather x0 -> x1, blocking collectives: none -> 71 us  [gather_native(): return [lax.all_gather(p, AXES, axis=0, tiled=False) for p in pieces]]
    all_gather x6 -> x4, waiting for transfers between devices: 178 us -> 131 us  [gather_native(): return [lax.all_gather(p, AXES, axis=0, tiled=False) for p in pieces]]
    pallas_call x0 -> x2, Pallas kernels: none -> 40.2 us  [the longest x1 22.3 us: attention_backward(): pl.pallas_call(functools.partial(attention_backward_kernel, chunk), grid_...]
    unnamed x81 -> x38, local copies, waits for them, and re-layouts: 41.9 us -> 11.2 us
  transfers between devices with their start and end apart: 12 -> 9, of which waited for: 9 -> 8; matrix products, arithmetic and copies ran while one was open for 28% -> 8% of each run, Pallas kernels for 0% -> 2%
where the time goes in v1:
time: 979 us; the launch traced here: 978 us
  waiting for transfers between devices  721 us (74%)
  matrix products  97 us (10%)
  blocking collectives  71 us (7%)
  Pallas kernels  40.2 us (4%)
  local copies, waits for them, and re-layouts  20.8 us (2%)
  between operations  14.3 us (1%)
  other arithmetic  12.9 us (1%)
    reduce_scatter x5, waiting for transfers between devices, reduce_native(): lax.psum_scatter(t.astype(F32), AXES, scatter_dimension=0, tiled=False)  588 us
    all_gather x4, waiting for transfers between devices, gather_native(): return [lax.all_gather(p, AXES, axis=0, tiled=False) for p in pieces]  131 us
    all_gather x1, blocking collectives, gather_native(): return [lax.all_gather(p, AXES, axis=0, tiled=False) for p in pieces]  71 us
    dot_general x4, matrix products, tn(): lax.dot_general(left, right, (((0,), (0,)), ((), ())), preferred_element_...  34.4 us
    dot_general x4, matrix products, nn(): return jnp.dot(left, right, preferred_element_type=F32)  32.1 us
    dot_general x4, matrix products, nt(): lax.dot_general(left, right, (((1,), (1,)), ((), ())), preferred_element_...  30.5 us
    pallas_call x1, Pallas kernels, attention_backward(): pl.pallas_call(functools.partial(attention_backward_kernel, chunk), grid_...  22.3 us
  transfers between devices with their start and end apart: 9, of which 8 were waited for; matrix products, arithmetic and copies ran while one was open for 8% of the time, Pallas kernels for 2%

profile of v1, /device:TPU:0, one launch (start us, length us, event | category | flops | bytes accessed | tf_op | source)
XLA Modules:
  0.0 977.8 jit_solution(17055824679924100235)
XLA Ops:
  7.2 1.6 pad_maximum_fusion.1
  8.9 0.7 all-gather.12.cloned.1.call-update
  9.6 0.7 all-gather.14.cloned.1.call-update
  10.4 0.5 all-gather.16.cloned.1.call-update
  10.9 0.7 reshape.168
  11.7 0.8 concatenate.17
  12.5 71.0 %all-gather.1 = bf16[512,128]{1,0:T(8,128)(2,1)S(1)} all-gather(bf16[16,128]{1,0:T(8,128)(2,1)S(1)} %pad.8), channel_id=3, replica_groups=mesh['fsdp'=8,'rep'=4] {'fsdp','rep'}, dimensions={0}, use_global_device_ids=true | all-gather | bytes 135168 | tf_op jit(solution)/shard_map/all_gather | solution.py:186
  83.6 0.1 squeeze.30
  83.7 0.1 squeeze.31
  83.8 0.1 add.113
  83.9 0.1 mul.138
  84.0 0.1 add.117
  84.1 0.1 add.120
  84.2 0.1 add.126
  84.3 0.1 mul.149
  84.4 2.1 convert_reduce_fusion.1
  86.5 0.1 add.130
  86.6 0.1 stack.66
  86.8 7.4 fusion.4.q_ref.k_ref.v_ref
  94.2 17.9 %attention_forward.1 = (bf16[1024,768]{1,0:T(8,128)(2,1)}, f32[2,6,2,512]{3,2,1,0:T(2,128)}) custom-call(s32[2]{0:T(128)} %len_ref.3, bf16[1024,2304]{1,0:T(8,128)(2,1)} %fusion.4.q_ref.k_ref.v_ref, bf16[1024,2304]{1,0:T(8,128)(2,1)} %fusion.4.q_ref.k_ref.v_ref, bf16[1024,2304]{1,0:T(8,128)(2,1)} %fusion.4.q_ref.k_ref.v_ref), custom_call_target="tpu_custom_call" | custom-call | tf_op jit(solution)/shard_map/attention_forward/pallas_call | solution.py:78
  112.1 17.7 %all-gather.12.cloned.1.call-done = bf16[768,768]{1,0:T(8,128)(2,1)} async-done(((bf16[24,768]{1,0:T(8,128)(2,1)}), bf16[768,768]{1,0:T(8,128)(2,1)}) %all-gather.12.cloned.1.call-update) | async-done | bytes 1179664 | tf_op jit(solution)/shard_map/all_gather | solution.py:186
  129.9 3.8 fusion.26
  133.6 0.5 multiply_reduce_fusion.3
  134.1 61.1 %all-gather.14.cloned.1.call-done = bf16[768,3072]{1,0:T(8,128)(2,1)} async-done(((bf16[24,3072]{1,0:T(8,128)(2,1)}), bf16[768,3072]{1,0:T(8,128)(2,1)}) %all-gather.14.cloned.1.call-update) | async-done | bytes 4718608 | tf_op jit(solution)/shard_map/all_gather | solution.py:186
  195.2 12.1 %multiply_convert_fusion.1 = (bf16[1024,3072]{1,0:T(8,128)(2,1)}, f32[1024,3072]{1,0:T(8,128)}) fusion(f32[3072]{0:T(1024)S(1)} %add.120, bf16[768,3072]{1,0:T(8,128)(2,1)} %all-gather.14.cloned.1.call-done, f32[1024,768]{1,0:T(8,128)S(1)} %get-tuple-element.60, f32[768]{0:T(1024)S(1)} %add.117, f32[768]{0:T(1024)S(1)} %mul.138, ...), kind=kOutput, calls=%fused_computation.7 | convolution fusion | flops 4854644736 | bytes 26765312 | tf_op jit(solution)/shard_map/dot_general | solution.py:22
  207.3 52.5 %all-gather.16.cloned.1.call-done = bf16[3072,768]{1,0:T(8,128)(2,1)} async-done(((bf16[96,768]{1,0:T(8,128)(2,1)}), bf16[3072,768]{1,0:T(8,128)(2,1)}) %all-gather.16.cloned.1.call-update) | async-done | bytes 4718608 | tf_op jit(solution)/shard_map/all_gather | solution.py:186
  259.8 8.8 fusion.27
  268.7 0.5 multiply_reduce_fusion.2
  269.2 0.9 copy-done
  270.0 1.3 fusion.11
  271.3 2.3 convert_reduce_fusion.2
  273.7 0.6 copy-done.7
  274.2 13.4 %convert_reduce_fusion = (f32[3072]{0:T(1024)S(1)}, bf16[1024,3072]{1,0:T(8,128)(2,1)S(1)}) fusion(f32[1024,3072]{1,0:T(8,128)} %get-tuple-element.62, f32[3072]{0:T(1024)S(1)} %add.120, bf16[3072,768]{1,0:T(8,128)(2,1)S(1)} %copy-done.7, f32[1024,768]{1,0:T(8,128)S(1)} %get-tuple-element.36), kind=kOutput, calls=%fused_computation.5 | convolution fusion | flops 4879807488 | bytes 26763264 | tf_op jit(solution)/shard_map/dot_general | solution.py:18
  287.7 6.0 multiply_reduce_fusion
  293.8 1.1 convert_reduce_fusion.3
  294.9 0.1 copy-done.10
  295.0 2.6 convolution_convert_fusion.g_ref
  297.6 22.3 %attention_backward.1 = (bf16[1024,768]{1,0:T(8,128)(2,1)}, bf16[1024,768]{1,0:T(8,128)(2,1)}, bf16[1024,768]{1,0:T(8,128)(2,1)}) custom-call(s32[2]{0:T(128)} %len_ref.3, bf16[1024,2304]{1,0:T(8,128)(2,1)} %fusion.4.q_ref.k_ref.v_ref, bf16[1024,2304]{1,0:T(8,128)(2,1)} %fusion.4.q_ref.k_ref.v_ref, bf16[1024,2304]{1,0:T(8,128)(2,1)} %fusion.4.q_ref.k_ref.v_ref, ...), custom_call_target="tpu_custom_call" | custom-call | tf_op jit(solution)/shard_map/attention_backward/pallas_call | solution.py:138
  319.9 1.7 convert_reduce_fusion.5
  321.6 2.9 constant_dynamic-update-slice_fusion.2
  324.5 1.7 convert_reduce_fusion.4
  326.2 0.1 stack.60
  326.7 0.1 reshape.178
  327.0 0.1 copy.45
  327.1 0.7 pad.9.clone
  327.9 2.9 constant_dynamic-update-slice_fusion.1
  330.9 1.3 constant_dynamic-update-slice_fusion
  332.1 8.3 fusion.28
  340.4 0.3 reduce-scatter.8.cloned.1.call-start
  340.7 5.2 fusion.13
  346.0 10.7 %fusion.19 = f32[768,3072]{1,0:T(8,128)} fusion(bf16[1024,3072]{1,0:T(8,128)(2,1)} %copy-done.1, f32[1024,768]{1,0:T(8,128)S(1)} %get-tuple-element.60, f32[768]{0:T(1024)S(1)} %add.117, f32[768]{0:T(1024)S(1)} %mul.138, f32[1024]{0:T(1024)S(1)} %add_rsqrt_fusion.1, f32[1024]{0:T(1024)S(1)} %broadcast_multiply_fusion.4), kind=kOutput, calls=%fused_computation.79 | convolution fusion | flops 4835770368 | bytes 18888704 | tf_op jit(solution)/shard_map/dot_general | solution.py:26
  356.8 1.8 copy-done.4
  358.6 10.2 %fusion.16 = f32[3072,768]{1,0:T(8,128)} fusion(bf16[1024,3072]{1,0:T(8,128)(2,1)} %get-tuple-element.61, f32[1024,768]{1,0:T(8,128)S(1)} %copy-done.4), kind=kOutput, calls=%fused_computation.76 | convolution fusion | flops 4832624640 | bytes 18874368 | tf_op jit(solution)/shard_map/dot_general | solution.py:26
  368.8 1.9 copy-done.6
  370.7 8.5 add_convert_fusion.1
  379.2 82.8 %reduce-scatter.14.cloned.1.call-done = f32[1,16,128]{2,1,0:T(8,128)} async-done(((f32[32,16,128]{2,1,0:T(8,128)}), f32[1,16,128]{2,1,0:T(8,128)}) %reduce-scatter.14.cloned.1.call-update) | async-done | bytes 8208 | tf_op jit(solution)/shard_map/reduce_scatter | solution.py:190
  462.0 0.7 slice.122
  462.7 0.6 reshape.179
  463.3 1.5 slice_bitcast_fusion
  464.8 118.6 %reduce-scatter.6.cloned.1.call-done = f32[1,24,2304]{2,1,0:T(8,128)} async-done(((f32[32,24,2304]{2,1,0:T(8,128)}), f32[1,24,2304]{2,1,0:T(8,128)}) %reduce-scatter.6.cloned.1.call-update) | async-done | bytes 221200 | tf_op jit(solution)/shard_map/reduce_scatter | solution.py:190
  583.4 1.6 fusion.24
  585.0 102.9 %reduce-scatter.8.cloned.1.call-done = f32[1,24,768]{2,1,0:T(8,128)} async-done(((f32[32,24,768]{2,1,0:T(8,128)}), f32[1,24,768]{2,1,0:T(8,128)}) %reduce-scatter.8.cloned.1.call-update) | async-done | bytes 73744 | tf_op jit(solution)/shard_map/reduce_scatter | solution.py:190
  687.9 141.7 %reduce-scatter.10.cloned.1.call-done = f32[1,24,3072]{2,1,0:T(8,128)} async-done(((f32[32,24,3072]{2,1,0:T(8,128)}), f32[1,24,3072]{2,1,0:T(8,128)}) %reduce-scatter.10.cloned.1.call-update) | async-done | bytes 294928 | tf_op jit(solution)/shard_map/reduce_scatter | solution.py:190
  829.6 141.6 %reduce-scatter.12.cloned.1.call-done = f32[1,96,768]{2,1,0:T(8,128)} async-done(((f32[32,96,768]{2,1,0:T(8,128)}), f32[1,96,768]{2,1,0:T(8,128)}) %reduce-scatter.12.cloned.1.call-update) | async-done | bytes 294928 | tf_op jit(solution)/shard_map/reduce_scatter | solution.py:190
  (68 shorter events, 1.1 us)
Async XLA Ops:
  7.2 79.6 %copy-start.8 = (bf16[2,512,768]{2,1,0:T(8,128)(2,1)S(1)}, bf16[2,512,768]{2,1,0:T(8,128)(2,1)}, u32[]{:S(2)}) copy-start(bf16[2,512,768]{2,1,0:T(8,128)(2,1)} %param.18) | copy-start | bytes 4718596
  7.2 79.5 %all-gather.10.cloned.1.call-start = ((), (), s32[]{:S(2)}) async-start(), calls=%async_computation.10 | async-start | bytes 3649536 | tf_op jit(solution)/shard_map/all_gather | solution.py:186
  8.8 121.0 %all-gather.12.cloned.1.call-start = ((), (), s32[]{:S(2)}) async-start(), calls=%async_computation.11 | async-start | bytes 1216512 | tf_op jit(solution)/shard_map/all_gather | solution.py:186
  9.6 185.6 %all-gather.14.cloned.1.call-start = ((), (), s32[]{:S(2)}) async-start(), calls=%async_computation.12 | async-start | bytes 4866048 | tf_op jit(solution)/shard_map/all_gather | solution.py:186
  10.3 249.5 %all-gather.16.cloned.1.call-start = ((), (), s32[]{:S(2)}) async-start(), calls=%async_computation.13 | async-start | bytes 4866048 | tf_op jit(solution)/shard_map/all_gather | solution.py:186
  10.9 451.1 %reduce-scatter.14.cloned.1.call-start = ((), (), s32[]{:S(2)}) async-start(), calls=%async_computation.9 | async-start | bytes 270336 | tf_op jit(solution)/shard_map/reduce_scatter | solution.py:190
  268.6 1.4 copy-start
  271.3 2.9 copy-start.7
  271.3 16.4 %slice-start = ((s8[4718592]{0:T(1024)(128)(4,1)}), s8[4194304]{0:T(1024)(128)(4,1)S(1)}, s32[]{:S(2)}) async-start(s8[4718592]{0:T(1024)(128)(4,1)} %bitcast.104), calls=%async_computation.14 | async-start | bytes 8388608
  273.7 14.0 %copy-start.3 = (f32[1024,768]{1,0:T(8,128)}, f32[1024,768]{1,0:T(8,128)S(1)}, u32[]{:S(2)}) copy-start(f32[1024,768]{1,0:T(8,128)S(1)} %get-tuple-element.36) | copy-start | bytes 9437188
  274.2 13.5 %slice-start.1 = ((s8[4718592]{0:T(1024)(128)(4,1)}), s8[524288]{0:T(1024)(128)(4,1)S(1)}, s32[]{:S(2)}) async-start(s8[4718592]{0:T(1024)(128)(4,1)} %bitcast.104), calls=%async_computation.15 | async-start | bytes 1048576
  287.7 6.1 copy-start.1
  293.8 1.3 copy-start.10
  294.9 2.7 copy-start.5
  327.9 255.5 %reduce-scatter.6.cloned.1.call-start = ((), (), s32[]{:S(2)}) async-start(), calls=%async_computation.5 | async-start | bytes 7299072 | tf_op jit(solution)/shard_map/reduce_scatter | solution.py:190
  327.9 2.9 copy-start.2
  327.9 4.2 copy-start.9
  340.4 347.5 %reduce-scatter.8.cloned.1.call-start = ((), (), s32[]{:S(2)}) async-start(), calls=%async_computation.6 | async-start | bytes 2433024 | tf_op jit(solution)/shard_map/reduce_scatter | solution.py:190
  346.0 483.6 %reduce-scatter.10.cloned.1.call-start = ((), (), s32[]{:S(2)}) async-start(), calls=%async_computation.7 | async-start | bytes 9732096 | tf_op jit(solution)/shard_map/reduce_scatter | solution.py:190
  356.7 1.9 copy-start.4
  356.7 614.5 %reduce-scatter.12.cloned.1.call-start = ((), (), s32[]{:S(2)}) async-start(), calls=%async_computation.8 | async-start | bytes 9732096 | tf_op jit(solution)/shard_map/reduce_scatter | solution.py:190
  368.8 1.9 copy-start.6
Sparse Core Ops, SparseCore 0:
  11.4 62.8 all-gather.9
  77.1 52.7 all-gather.11
  132.7 62.5 all-gather.13
  197.9 61.8 all-gather.15
  328.0 133.9 reduce-scatter.13
  467.5 115.8 reduce-scatter.5
  589.3 98.6 reduce-scatter.7
  694.4 135.1 reduce-scatter.9
  836.1 135.0 reduce-scatter.11
